TPU v7x, 32 devices: a whole 2x2x4 slice. The times are simulated.
32 devices in a mesh: seq: 4 (over y, x), batch: 8 (over z, core).
Axes of the slice: x: 2, y: 2, z: 4, core: 2. Of those that a mesh axis runs over, the one named last changes fastest.
Arguments:
- activations: bfloat16 [8, 3072, 4096], P('batch', 'seq'), may hold values from -18 to 18
- out_grads: bfloat16 [8, 3072, 4096], P('batch', 'seq'), may hold values from -0.29882812 to 0.29882812
- lengths: int32 [8, 3], P('batch'), may hold values from 1 to 1536, 3072 in all within a row
Outputs:
- act_factor: float32 [4096, 4096], P(('seq', 'batch'))
- grad_factor: float32 [4096, 4096], P(('seq', 'batch'))
Inputs may be any that keep to these rules, and one draw needn't show every extreme that they name: `lengths`: each row sums to 3072 and its largest entry is exactly 1536.
All inputs are finite; a program needn't handle non-finite values.
Results may differ from a plain program's by a relative error of at most 0.004.
Values may be sent and summed in bfloat16 or wider, within the bound.
A program may use at most 64 MiB of HBM per device.

v0:
```python
import jax
import jax.numpy as jnp
from jax import lax
from jax.sharding import PartitionSpec as P


def local(activations, out_grads, lengths):
    act_local = activations[0]
    grad_local = out_grads[0]
    seq_lengths = lengths[0]
    tok_count = act_local.shape[0]
    width = act_local.shape[1]
    seq_count = seq_lengths.shape[0]
    group_size = lax.axis_size("seq")
    devices = group_size * lax.axis_size("batch")
    tile_rows = width // devices
    tile_start = lax.axis_index(("seq", "batch")) * tile_rows
    total_seqs = seq_count * lax.axis_size("batch")
    ends = jnp.cumsum(seq_lengths)
    starts = ends - seq_lengths
    position = lax.axis_index("seq") * tok_count + jnp.arange(tok_count, dtype=jnp.int32)
    member = (position[None, :] >= starts[:, None]) & (position[None, :] < ends[:, None])
    member = member.astype(jnp.bfloat16)
    act_part = jnp.dot(member, act_local, preferred_element_type=jnp.float32)
    grad_part = jnp.dot(member, grad_local, preferred_element_type=jnp.float32)
    act_sum, grad_sum = lax.psum((act_part, grad_part), "seq")
    act_rows = (act_sum / seq_lengths[:, None].astype(jnp.float32)).astype(jnp.bfloat16)
    grad_rows = grad_sum.astype(jnp.bfloat16)
    act_piece = lax.all_gather(act_rows, "batch", axis=0, tiled=True)
    grad_piece = lax.all_gather(grad_rows, "batch", axis=0, tiled=True)
    act_cols = lax.dynamic_slice_in_dim(act_piece, tile_start, tile_rows, 1)
    grad_cols = lax.dynamic_slice_in_dim(grad_piece, tile_start, tile_rows, 1)
    dims = (((0,), (0,)), ((), ()))
    act_new = lax.dot_general(act_cols, act_piece, dims, preferred_element_type=jnp.float32)
    grad_new = lax.dot_general(grad_cols, grad_piece, dims, preferred_element_type=jnp.float32)
    return (act_new / total_seqs, grad_new / total_seqs)


def solution(mesh):
    in_specs = (P("batch", "seq", None), P("batch", "seq", None), P("batch", None))
    out_specs = (P(("seq", "batch"), None), P(("seq", "batch"), None))
    return jax.shard_map(local, mesh=mesh, in_specs=in_specs, out_specs=out_specs, check_vma=False)
```

profile of v0, /device:TPU:0, one launch (start us, length us, event | category | flops | bytes accessed | tf_op | source)
XLA Modules:
  0.0 60.4 jit_solution(18398643600127713620)
XLA Ops:
  0.6 0.8 %reduce-window.7 = s32[3,1]{0,1:T(1,128)S(1)} reduce-window(s32[3,1]{0,1:T(1,128)} %bitcast.22, s32[]{:T(128)} %constant.7.clone.1), window={size=3x1 pad=2_0x0_0}, to_apply=%region_0.0 | reduce-window | flops 6 | bytes 28 | tf_op jit(solution)/shard_map/reduce-window.2
  1.5 0.0 copy-start
  1.5 0.8 %bitcast_subtract_fusion = s32[3]{0:T(128)S(1)} fusion(s32[1,3]{1,0:T(1,128)} %param.5, s32[3,1]{0,1:T(1,128)S(1)} %reduce-window.7), kind=kLoop, calls=%fused_computation.14 | loop fusion | flops 3 | bytes 36 | tf_op jit(solution)/shard_map/sub | solution.py:20
  2.3 0.8 %bitcast_convert_fusion = f32[3]{0:T(128)S(1)} fusion(s32[1,3]{1,0:T(1,128)} %param.5), kind=kLoop, calls=%fused_computation.13 | loop fusion | flops 3 | bytes 24 | tf_op jit(solution)/shard_map/convert_element_type | solution.py:27
  3.1 4.0 %fusion = f32[3,4096]{1,0:T(4,128)S(1)} fusion(bf16[1,768,4096]{2,1,0:T(8,128)(2,1)} %param.4, s32[768]{0:T(1024)S(1)} %iota_add_fusion, s32[3]{0:T(128)S(1)} %bitcast.20, s32[3]{0:T(128)S(1)} %bitcast_subtract_fusion), kind=kOutput, calls=%fused_computation | convolution fusion | flops 18881280 | bytes 6343704 | tf_op jit(solution)/shard_map/dot_general | solution.py:25
  7.1 0.0 copy-done
  7.1 1.0 %fusion.2 = f32[3,4096]{1,0:T(4,128)S(1)} fusion(bf16[1,768,4096]{2,1,0:T(8,128)(2,1)S(1)} %copy-done, s32[768]{0:T(1024)S(1)} %iota_add_fusion, s32[3]{0:T(128)S(1)} %bitcast.21, s32[3]{0:T(128)S(1)} %bitcast_subtract_fusion), kind=kOutput, calls=%fused_computation.2 | convolution fusion | flops 18881280 | bytes 6343704 | tf_op jit(solution)/shard_map/dot_general | solution.py:24
  8.0 19.8 %all-reduce.2 = (f32[3,4096]{1,0:T(4,128)S(1)}, bf16[3,4096]{1,0:T(4,128)(2,1)S(1)}) all-reduce(f32[3,4096]{1,0:T(4,128)S(1)} %fusion.2, f32[3,4096]{1,0:T(4,128)S(1)} %fusion), channel_id=1, replica_groups=mesh['seq'=4,'batch'=8] {'seq'}, use_global_device_ids=true, to_apply=%region_1.2 | all-reduce | flops 24576 | bytes 172032 | tf_op jit(solution)/shard_map/psum | solution.py:26
  27.8 0.1 fusion.4
  27.9 14.4 %all-gather.1 = bf16[8,3,4096]{2,1,0:T(4,128)(2,1)S(1)} all-gather(bf16[1,3,4096]{2,1,0:T(4,128)(2,1)S(1)} %bitcast.19), channel_id=1, replica_groups=mesh['seq'=4,'batch'=8] {'batch'}, dimensions={0}, use_global_device_ids=true | all-gather | bytes 221184 | tf_op jit(solution)/shard_map/all_gather | solution.py:30
  42.3 0.2 reshape.48
  42.5 14.2 %all-gather = bf16[8,3,4096]{2,1,0:T(4,128)(2,1)S(1)} all-gather(bf16[1,3,4096]{2,1,0:T(4,128)(2,1)S(1)} %fusion.4), channel_id=1, replica_groups=mesh['seq'=4,'batch'=8] {'batch'}, dimensions={0}, use_global_device_ids=true | all-gather | bytes 221184 | tf_op jit(solution)/shard_map/all_gather | solution.py:29
  56.7 0.2 reshape.46
  56.9 1.8 %convolution_multiply_fusion.1 = f32[128,4096]{1,0:T(8,128)} fusion(bf16[24,4096]{1,0:T(8,128)(2,1)S(1)} %reshape.46, s32[]{:T(128)S(6)} %select_n.4), kind=kOutput, calls=%fused_computation.5 | convolution fusion | flops 25690112 | bytes 2299908 | tf_op jit(solution)/shard_map/dot_general | solution.py:34
  58.7 1.8 %convolution_multiply_fusion = f32[128,4096]{1,0:T(8,128)} fusion(bf16[24,4096]{1,0:T(8,128)(2,1)S(1)} %reshape.48, s32[]{:T(128)S(6)} %select_n.4), kind=kOutput, calls=%fused_computation.4 | convolution fusion | flops 25690112 | bytes 2299908 | tf_op jit(solution)/shard_map/dot_general | solution.py:35
  (1 shorter events, 0.0 us)
Async XLA Ops:
  1.5 5.6 %copy-start = (bf16[1,768,4096]{2,1,0:T(8,128)(2,1)S(1)}, bf16[1,768,4096]{2,1,0:T(8,128)(2,1)}, u32[]{:S(2)}) copy-start(bf16[1,768,4096]{2,1,0:T(8,128)(2,1)} %param.3) | copy-start | bytes 18874372
where the time goes:
time: 60.7 us; the launch traced here: 60.4 us
  blocking collectives  48.4 us (80%)
  matrix products  8.53 us (14%)
  other arithmetic  2.51 us (4%)
  between operations  0.67 us (1%)
    psum x1, blocking collectives, local(): act_sum, grad_sum = lax.psum((act_part, grad_part), 'seq')  19.8 us
    all_gather x1, blocking collectives, local(): grad_piece = lax.all_gather(grad_rows, 'batch', axis=0, tiled=True)  14.4 us
    all_gather x1, blocking collectives, local(): act_piece = lax.all_gather(act_rows, 'batch', axis=0, tiled=True)  14.2 us
    dot_general x1, matrix products, local(): grad_part = jnp.dot(member, grad_local, preferred_element_type=jnp.float32)  3.99 us
    dot_general x1, matrix products, local(): lax.dot_general(act_cols, act_piece, dims, preferred_element_type=jnp.flo...  1.79 us
    dot_general x1, matrix products, local(): lax.dot_general(grad_cols, grad_piece, dims, preferred_element_type=jnp.f...  1.78 us

commit v1 on v0

v1 whole, which is shorter than its diff:
```python
import functools

import jax
import jax.numpy as jnp
from jax import lax
from jax.experimental import pallas as pl
from jax.experimental.pallas import tpu as pltpu
from jax.sharding import PartitionSpec as P

MESH = pl.DeviceIdType.MESH


def gather_kernel(S, B, count, len_ref, act_hbm, grad_hbm, gath, tokens, part, landed,
                  read_sem, rs_send, rs_recv, z_send, z_recv, p_send, p_recv, c_send, c_recv):
    Z = B // 2
    q = lax.axis_index("seq")
    b = lax.axis_index("batch")
    z, core = b // 2, b % 2
    T, D = act_hbm.shape[1:]
    cols = D // S
    R = part.shape[2]
    sources = (act_hbm, grad_hbm)
    order = tuple(range(1, S)) + (0,)

    def span(owner):
        return pl.ds(pl.multiple_of(owner * cols, cols), cols)

    def seq_at(k):
        return lax.rem(q + k, S)

    def z_at(j):
        return lax.rem(z + j, Z)

    def read(t, k):
        s = span(seq_at(k))
        return pltpu.make_async_copy(sources[t].at[0, :, s], tokens.at[t, :, s], read_sem.at[t, k])

    for t in range(2):
        for k in order:
            read(t, k).start()

    seq_peers = [{"seq": seq_at(k)} for k in range(1, S)]
    z_peers = [{"batch": z_at(j) * 2 + core} for j in range(1, Z)]
    other = {"batch": z * 2 + 1 - core}
    barrier = pltpu.get_barrier_semaphore()
    everyone = seq_peers + z_peers + [other]
    for peer in everyone:
        pl.semaphore_signal(barrier, inc=1, device_id=peer, device_id_type=MESH)

    row = lax.broadcasted_iota(jnp.int32, (8, T), 0)
    position = q * T + lax.broadcasted_iota(jnp.int32, (8, T), 1)
    first = jnp.zeros((8, T), jnp.int32)
    last = jnp.zeros((8, T), jnp.int32)
    begin = 0
    for s in range(count):
        end = begin + len_ref[0, s]
        first = jnp.where(row == s, begin, first)
        last = jnp.where(row == s, end, last)
        begin = end
    member = ((position >= first) & (position < last)).astype(jnp.float32).astype(jnp.bfloat16)

    which = lax.broadcasted_iota(jnp.int32, (R, cols), 0)
    sizes = jnp.ones((R, cols), jnp.float32)
    for s in range(count):
        sizes = jnp.where(which == s, len_ref[0, s].astype(jnp.float32), sizes)

    def scatter(t, k):
        return pltpu.make_async_remote_copy(
            src_ref=part.at[t, k], dst_ref=landed.at[t, k - 1],
            send_sem=rs_send.at[t, k - 1], recv_sem=rs_recv.at[t, k - 1],
            device_id=seq_peers[k - 1], device_id_type=MESH)

    def to_z(t, j):
        block = gath.at[t, core, z, :, span(q)]
        return pltpu.make_async_remote_copy(
            src_ref=block, dst_ref=block, send_sem=z_send.at[t, j - 1], recv_sem=z_recv.at[t, j - 1],
            device_id=z_peers[j - 1], device_id_type=MESH)

    def from_z(t, j):
        block = gath.at[t, core, z_at(Z - j), :, span(q)]
        return pltpu.make_async_remote_copy(
            src_ref=block, dst_ref=block, send_sem=z_send.at[t, j - 1], recv_sem=z_recv.at[t, j - 1],
            device_id=z_peers[j - 1], device_id_type=MESH)

    def to_plane(t, k, zz):
        block = gath.at[t, core, zz, :, span(q)]
        return pltpu.make_async_remote_copy(
            src_ref=block, dst_ref=block, send_sem=p_send.at[t, k - 1], recv_sem=p_recv.at[t, k - 1],
            device_id=seq_peers[k - 1], device_id_type=MESH)

    def plane_group(t, k, owner):
        block = gath.at[t, core, :, :, span(owner)]
        return pltpu.make_async_remote_copy(
            src_ref=block, dst_ref=block, send_sem=p_send.at[t, k - 1], recv_sem=p_recv.at[t, k - 1],
            device_id=seq_peers[k - 1], device_id_type=MESH)

    def to_core(t, k, side):
        block = gath.at[t, side, :, :, span(seq_at(S - k))]
        return pltpu.make_async_remote_copy(
            src_ref=block, dst_ref=block, send_sem=c_send.at[t, k], recv_sem=c_recv.at[t, k],
            device_id=other, device_id_type=MESH)

    for t in range(2):
        for k in order:
            read(t, k).wait()
            block = tokens[t, :, span(seq_at(k))]
            sums = jnp.dot(member, block, preferred_element_type=jnp.float32)
            part[t, k] = sums[:R]
            if t == 0 and k == order[0]:
                pl.semaphore_wait(barrier, len(everyone))
            if k:
                scatter(t, k).start()

    for t in range(2):
        total = part[t, 0]
        for k in range(1, S):
            scatter(t, k).wait_recv()
            total = total + landed[t, k - 1]
        if t == 0:
            total = total / sizes
        gath[t, core, z, :, span(q)] = total.astype(jnp.bfloat16)
        for j in range(1, Z):
            to_z(t, j).start()
        for k in range(1, S):
            to_plane(t, k, z).start()

    for t in range(2):
        for j in range(1, Z):
            from_z(t, j).wait_recv()
            for k in range(1, S):
                to_plane(t, k, z_at(Z - j)).start()
        to_core(t, 0, core).start()

    for t in range(2):
        for k in range(1, S):
            plane_group(t, k, seq_at(S - k)).wait_recv()
            to_core(t, k, core).start()

    for t in range(2):
        for k in range(S):
            to_core(t, k, 1 - core).wait_recv()
    for t in range(2):
        for k in range(S):
            to_core(t, k, core).wait_send()
        for k in range(1, S):
            scatter(t, k).wait_send()
            plane_group(t, k, q).wait_send()
        for j in range(1, Z):
            to_z(t, j).wait_send()


def outer_kernel(total, tile, steps, gath, act_out, grad_out, tiles, sem):
    D = gath.shape[-1]
    K = gath.shape[1] * gath.shape[2] * gath.shape[3]
    me = lax.axis_index("seq") * lax.axis_size("batch") + lax.axis_index("batch")
    at = me * tile
    width = D // steps
    outs = (act_out, grad_out)
    dims = (((0,), (0,)), ((), ()))
    wide = max(tile, 128)

    def rows(t, s):
        return gath[t, :, :, :, s].reshape(K, -1)

    def put(t, c):
        s = pl.ds(c * width, width)
        return pltpu.make_async_copy(tiles.at[t, :, s], outs[t].at[:, s], sem.at[t, c])

    for t in range(2):
        if tile % 128 == 0:
            mine = rows(t, pl.ds(pl.multiple_of(at, 128), tile))
        else:
            block = rows(t, pl.ds(pl.multiple_of(at // wide * wide, wide), wide))
            pick = lax.broadcasted_iota(jnp.int32, (wide, tile), 0) == at % wide + lax.broadcasted_iota(jnp.int32, (wide, tile), 1)
            mine = jnp.dot(block, pick.astype(jnp.float32).astype(jnp.bfloat16), preferred_element_type=jnp.float32).astype(jnp.bfloat16)
        for c in range(steps):
            s = pl.ds(c * width, width)
            new = lax.dot_general(mine, rows(t, s), dims, preferred_element_type=jnp.float32)
            tiles[t, :, s] = new * (1.0 / total)
            put(t, c).start()
    for t in range(2):
        for c in range(steps):
            put(t, c).wait()


def solution(mesh):
    S, B = mesh.shape["seq"], mesh.shape["batch"]
    Z = B // 2

    def local(activations, out_grads, lengths):
        T, D = activations.shape[1:]
        count = lengths.shape[1]
        R = max(2, 1 << (count - 1).bit_length())
        cols = D // S
        tile = D // (S * B)
        steps = 4
        gath = pl.pallas_call(
            functools.partial(gather_kernel, S, B, count),
            out_shape=jax.ShapeDtypeStruct((2, 2, Z, R, D), jnp.bfloat16),
            in_specs=[pl.BlockSpec(memory_space=pltpu.SMEM), pl.BlockSpec(memory_space=pl.ANY), pl.BlockSpec(memory_space=pl.ANY)],
            out_specs=pl.BlockSpec(memory_space=pltpu.VMEM),
            scratch_shapes=[
                pltpu.VMEM((2, T, D), jnp.bfloat16),
                pltpu.VMEM((2, S, R, cols), jnp.float32),
                pltpu.VMEM((2, S - 1, R, cols), jnp.float32),
                pltpu.SemaphoreType.DMA((2, S)),
                pltpu.SemaphoreType.DMA((2, S - 1)),
                pltpu.SemaphoreType.DMA((2, S - 1)),
                pltpu.SemaphoreType.DMA((2, Z - 1)),
                pltpu.SemaphoreType.DMA((2, Z - 1)),
                pltpu.SemaphoreType.DMA((2, S - 1)),
                pltpu.SemaphoreType.DMA((2, S - 1)),
                pltpu.SemaphoreType.DMA((2, S)),
                pltpu.SemaphoreType.DMA((2, S)),
            ],
            compiler_params=pltpu.CompilerParams(collective_id=0, has_side_effects=True),
            name="gather_rows",
        )(lengths, activations, out_grads)
        out = jax.ShapeDtypeStruct((tile, D), jnp.float32)
        return tuple(pl.pallas_call(
            functools.partial(outer_kernel, count * B, tile, steps),
            out_shape=(out, out),
            in_specs=[pl.BlockSpec(memory_space=pltpu.VMEM)],
            out_specs=(pl.BlockSpec(memory_space=pl.ANY), pl.BlockSpec(memory_space=pl.ANY)),
            scratch_shapes=[pltpu.VMEM((2, tile, D), jnp.float32), pltpu.SemaphoreType.DMA((2, steps))],
            name="outer_rows",
        )(gath))

    in_specs = (P("batch", "seq", None), P("batch", "seq", None), P("batch", None))
    out_specs = (P(("seq", "batch"), None), P(("seq", "batch"), None))
    return jax.shard_map(local, mesh=mesh, in_specs=in_specs, out_specs=out_specs, check_vma=False)
```

time: 60.7 us -> 25.2 us (0.42)
  blocking collectives: 48.4 us -> 0 us
  Pallas kernels: 0 us -> 24.4 us
  matrix products: 8.53 us -> 0 us
  other arithmetic: 2.51 us -> 0 us
    all_gather x2 -> x0, blocking collectives: 28.6 us -> none  [the longest x1 14.4 us: local(): grad_piece = lax.all_gather(grad_rows, 'batch', axis=0, tiled=True)]
    pallas_call x0 -> x2, Pallas kernels: none -> 24.4 us  [the longest x1 21.1 us: local(): pl.pallas_call(functools.partial(gather_kernel, S, B, count), out_shape=j...]
    psum x1 -> x0, blocking collectives: 19.8 us -> none  [local(): act_sum, grad_sum = lax.psum((act_part, grad_part), 'seq')]
    dot_general x4 -> x0, matrix products: 8.53 us -> none  [the longest x1 3.99 us: local(): grad_part = jnp.dot(member, grad_local, preferred_element_type=jnp.float32)]
    another operation x1 -> x0, other arithmetic: 0.83 us -> none
    sub x1 -> x0, other arithmetic: 0.81 us -> none  [local(): starts = ends - seq_lengths]
    convert_element_type x1 -> x0, other arithmetic: 0.78 us -> none  [local(): seq_lengths[:, None].astype(jnp.float32)]
where the time goes in v1:
time: 25.2 us; the launch traced here: 25.1 us
  Pallas kernels  24.4 us (97%)
  between operations  0.64 us (3%)
    pallas_call x1, Pallas kernels, local(): pl.pallas_call(functools.partial(gather_kernel, S, B, count), out_shape=j...  21.1 us
    pallas_call x1, Pallas kernels, local(): pl.pallas_call(functools.partial(outer_kernel, count * B, tile, steps), o...  3.38 us

profile of v1, /device:TPU:0, one launch (start us, length us, event | category | flops | bytes accessed | tf_op | source)
XLA Modules:
  0.0 25.1 jit_solution(17797824083007436034)
XLA Ops:
  0.6 21.1 %gather_rows.1.gath = bf16[2,2,4,4,4096]{4,3,2,1,0:T(4,128)(2,1)} custom-call(s32[1,3]{1,0:T(1,128)} %len_ref.1, bf16[1,768,4096]{2,1,0:T(8,128)(2,1)} %act_hbm.1, bf16[1,768,4096]{2,1,0:T(8,128)(2,1)} %grad_hbm.1), custom_call_target="tpu_custom_call" | custom-call | tf_op jit(solution)/shard_map/gather_rows/pallas_call | solution.py:197
  21.7 3.4 %outer_rows.1 = (f32[128,4096]{1,0:T(8,128)}, f32[128,4096]{1,0:T(8,128)}) custom-call(bf16[2,2,4,4,4096]{4,3,2,1,0:T(4,128)(2,1)} %gather_rows.1.gath), custom_call_target="tpu_custom_call" | custom-call | tf_op jit(solution)/shard_map/outer_rows/pallas_call | solution.py:220

commit v2 on v0

v2 whole, which is shorter than its diff:
```python
import functools

import jax
import jax.numpy as jnp
from jax import lax
from jax.experimental import pallas as pl
from jax.experimental.pallas import tpu as pltpu
from jax.sharding import PartitionSpec as P

MESH = pl.DeviceIdType.MESH


def factor_kernel(S, B, H, count, len_ref, act_hbm, grad_hbm, act_tile, grad_tile, gath, tokens, part, landed,
                  read_sem, rs_send, rs_recv, z_send, z_recv, p_send, p_recv, c_send, c_recv):
    Z = B // 2
    q = lax.axis_index("seq")
    b = lax.axis_index("batch")
    z, core = b // 2, b % 2
    T, D = act_hbm.shape[1:]
    cols = D // S
    width = cols // H
    R = part.shape[2]
    sources = (act_hbm, grad_hbm)
    tiles = (act_tile, grad_tile)
    tile = act_tile.shape[0]
    order = tuple(range(1, S)) + (0,)
    units = [(t, h) for t in range(2) for h in range(H)]

    def span(owner, h):
        return pl.ds(pl.multiple_of(owner * cols + h * width, width), width)

    def seq_at(k):
        return lax.rem(q + k, S)

    def z_at(j):
        return lax.rem(z + j, Z)

    def read(u, k):
        t, h = units[u]
        s = span(seq_at(k), h)
        return pltpu.make_async_copy(sources[t].at[0, :, s], tokens.at[t, :, s], read_sem.at[u, k])

    for u in range(len(units)):
        for k in order:
            read(u, k).start()

    seq_peers = [{"seq": seq_at(k)} for k in range(1, S)]
    z_peers = [{"batch": z_at(j) * 2 + core} for j in range(1, Z)]
    other = {"batch": z * 2 + 1 - core}
    barrier = pltpu.get_barrier_semaphore()
    everyone = seq_peers + z_peers + [other]
    for peer in everyone:
        pl.semaphore_signal(barrier, inc=1, device_id=peer, device_id_type=MESH)

    row = lax.broadcasted_iota(jnp.int32, (8, T), 0)
    position = q * T + lax.broadcasted_iota(jnp.int32, (8, T), 1)
    first = jnp.zeros((8, T), jnp.int32)
    last = jnp.zeros((8, T), jnp.int32)
    begin = 0
    for s in range(count):
        end = begin + len_ref[0, s]
        first = jnp.where(row == s, begin, first)
        last = jnp.where(row == s, end, last)
        begin = end
    member = ((position >= first) & (position < last)).astype(jnp.float32).astype(jnp.bfloat16)

    which = lax.broadcasted_iota(jnp.int32, (R, width), 0)
    sizes = jnp.ones((R, width), jnp.float32)
    for s in range(count):
        sizes = jnp.where(which == s, len_ref[0, s].astype(jnp.float32), sizes)

    def send(src, dst, send_sem, recv_sem, peer):
        return pltpu.make_async_remote_copy(
            src_ref=src, dst_ref=dst, send_sem=send_sem, recv_sem=recv_sem, device_id=peer, device_id_type=MESH)

    def scatter(u, k):
        return send(part.at[u, k], landed.at[u, k - 1], rs_send.at[u, k - 1], rs_recv.at[u, k - 1], seq_peers[k - 1])

    def at_z(u, j, zz):
        t, h = units[u]
        block = gath.at[t, core, zz, :, span(q, h)]
        return send(block, block, z_send.at[u, j - 1], z_recv.at[u, j - 1], z_peers[j - 1])

    def to_plane(u, k, zz):
        t, h = units[u]
        block = gath.at[t, core, zz, :, span(q, h)]
        return send(block, block, p_send.at[u, k - 1], p_recv.at[u, k - 1], seq_peers[k - 1])

    def plane_group(u, k, owner):
        t, h = units[u]
        block = gath.at[t, core, :, :, span(owner, h)]
        return send(block, block, p_send.at[u, k - 1], p_recv.at[u, k - 1], seq_peers[k - 1])

    def to_core(u, k, side):
        t, h = units[u]
        block = gath.at[t, side, :, :, span(seq_at(S - k), h)]
        return send(block, block, c_send.at[u, k], c_recv.at[u, k], other)

    for u, (t, h) in enumerate(units):
        for k in order:
            read(u, k).wait()
            sums = jnp.dot(member, tokens[t, :, span(seq_at(k), h)], preferred_element_type=jnp.float32)
            part[u, k] = sums[:R]
            if u == 0 and k == order[0]:
                pl.semaphore_wait(barrier, len(everyone))
            if k:
                scatter(u, k).start()

    for u, (t, h) in enumerate(units):
        total = part[u, 0]
        for k in range(1, S):
            scatter(u, k).wait_recv()
            total = total + landed[u, k - 1]
        if t == 0:
            total = total / sizes
        gath[t, core, z, :, span(q, h)] = total.astype(jnp.bfloat16)
        for j in range(1, Z):
            at_z(u, j, z).start()
        for k in range(1, S):
            to_plane(u, k, z).start()

    for u in range(len(units)):
        for j in range(1, Z):
            at_z(u, j, z_at(Z - j)).wait_recv()
            for k in range(1, S):
                to_plane(u, k, z_at(Z - j)).start()
        to_core(u, 0, core).start()

    K = gath.shape[1] * Z * R

    def rows(t, s):
        return gath[t, :, :, :, s].reshape(K, -1)

    wide = max(tile, 128)
    at = q * cols + b * tile

    for t in range(2):
        mine = [u for u in range(len(units)) if units[u][0] == t]
        for u in mine:
            for k in range(1, S):
                plane_group(u, k, seq_at(S - k)).wait_recv()
                to_core(u, k, core).start()
        for u in mine:
            to_core(u, 0, 1 - core).wait_recv()
        if tile % 128 == 0:
            block = rows(t, pl.ds(pl.multiple_of(at, 128), tile))
        else:
            block = rows(t, pl.ds(pl.multiple_of(at // wide * wide, wide), wide))
            pick = lax.broadcasted_iota(jnp.int32, (wide, tile), 0) == at % wide + lax.broadcasted_iota(jnp.int32, (wide, tile), 1)
            block = jnp.dot(block, pick.astype(jnp.float32).astype(jnp.bfloat16), preferred_element_type=jnp.float32).astype(jnp.bfloat16)
        left = block.T
        for u in mine:
            h = units[u][1]
            for k in range(S):
                if k:
                    to_core(u, k, 1 - core).wait_recv()
                s = span(seq_at(S - k), h)
                tiles[t][:, s] = jnp.dot(left, rows(t, s), preferred_element_type=jnp.float32) * (1.0 / (count * B))

    for u in range(len(units)):
        for k in range(S):
            to_core(u, k, core).wait_send()
        for k in range(1, S):
            scatter(u, k).wait_send()
            plane_group(u, k, q).wait_send()
        for j in range(1, Z):
            at_z(u, j, z).wait_send()


def solution(mesh):
    S, B = mesh.shape["seq"], mesh.shape["batch"]
    Z = B // 2

    def local(activations, out_grads, lengths):
        T, D = activations.shape[1:]
        count = lengths.shape[1]
        R = max(2, 1 << (count - 1).bit_length())
        cols = D // S
        tile = D // (S * B)
        H = 2
        U = 2 * H
        out = pltpu.VMEM((tile, D), jnp.float32)
        return tuple(pl.pallas_call(
            functools.partial(factor_kernel, S, B, H, count),
            out_shape=(out, out),
            in_specs=[pl.BlockSpec(memory_space=pltpu.SMEM), pl.BlockSpec(memory_space=pl.ANY), pl.BlockSpec(memory_space=pl.ANY)],
            out_specs=(pl.BlockSpec(memory_space=pltpu.VMEM), pl.BlockSpec(memory_space=pltpu.VMEM)),
            scratch_shapes=[
                pltpu.VMEM((2, 2, Z, R, D), jnp.bfloat16),
                pltpu.VMEM((2, T, D), jnp.bfloat16),
                pltpu.VMEM((U, S, R, cols // H), jnp.float32),
                pltpu.VMEM((U, S - 1, R, cols // H), jnp.float32),
                pltpu.SemaphoreType.DMA((U, S)),
                pltpu.SemaphoreType.DMA((U, S - 1)),
                pltpu.SemaphoreType.DMA((U, S - 1)),
                pltpu.SemaphoreType.DMA((U, Z - 1)),
                pltpu.SemaphoreType.DMA((U, Z - 1)),
                pltpu.SemaphoreType.DMA((U, S - 1)),
                pltpu.SemaphoreType.DMA((U, S - 1)),
                pltpu.SemaphoreType.DMA((U, S)),
                pltpu.SemaphoreType.DMA((U, S)),
            ],
            compiler_params=pltpu.CompilerParams(collective_id=0, has_side_effects=True, vmem_limit_bytes=56 * 2**20),
            name="factors",
        )(lengths, activations, out_grads))

    in_specs = (P("batch", "seq", None), P("batch", "seq", None), P("batch", None))
    out_specs = (P(("seq", "batch"), None), P(("seq", "batch"), None))
    return jax.shard_map(local, mesh=mesh, in_specs=in_specs, out_specs=out_specs, check_vma=False)
```

time: 60.7 us -> 25.5 us (0.42)
  blocking collectives: 48.4 us -> 0 us
  Pallas kernels: 0 us -> 22.1 us
  matrix products: 8.53 us -> 0 us
  other arithmetic: 2.51 us -> 0 us
  local copies, waits for them, and re-layouts: 0.34 us -> 2.64 us
    all_gather x2 -> x0, blocking collectives: 28.6 us -> none  [the longest x1 14.4 us: local(): grad_piece = lax.all_gather(grad_rows, 'batch', axis=0, tiled=True)]
    pallas_call x0 -> x1, Pallas kernels: none -> 22.1 us  [local(): pl.pallas_call(functools.partial(factor_kernel, S, B, H, count), out_shap...]
    psum x1 -> x0, blocking collectives: 19.8 us -> none  [local(): act_sum, grad_sum = lax.psum((act_part, grad_part), 'seq')]
    dot_general x4 -> x0, matrix products: 8.53 us -> none  [the longest x1 3.99 us: local(): grad_part = jnp.dot(member, grad_local, preferred_element_type=jnp.float32)]
    unnamed x4 -> x2, local copies, waits for them, and re-layouts: 0.34 us -> 2.64 us
    another operation x1 -> x0, other arithmetic: 0.83 us -> none
    sub x1 -> x0, other arithmetic: 0.81 us -> none  [local(): starts = ends - seq_lengths]
    convert_element_type x1 -> x0, other arithmetic: 0.78 us -> none  [local(): seq_lengths[:, None].astype(jnp.float32)]
where the time goes in v2:
time: 25.5 us; the launch traced here: 25.4 us
  Pallas kernels  22.1 us (87%)
  local copies, waits for them, and re-layouts  2.64 us (10%)
  between operations  0.64 us (3%)
    pallas_call x1, Pallas kernels, local(): pl.pallas_call(functools.partial(factor_kernel, S, B, H, count), out_shap...  22.1 us
    unnamed x2, local copies, waits for them, and re-layouts  2.64 us

profile of v2, /device:TPU:0, one launch (start us, length us, event | category | flops | bytes accessed | tf_op | source)
XLA Modules:
  0.0 25.4 jit_solution(5599691807430225680)
XLA Ops:
  0.6 22.1 %factors.1 = (f32[128,4096]{1,0:T(8,128)S(1)}, f32[128,4096]{1,0:T(8,128)S(1)}) custom-call(s32[1,3]{1,0:T(1,128)} %len_ref.1, bf16[1,768,4096]{2,1,0:T(8,128)(2,1)} %act_hbm.1, bf16[1,768,4096]{2,1,0:T(8,128)(2,1)} %grad_hbm.1), custom_call_target="tpu_custom_call" | custom-call | tf_op jit(solution)/shard_map/factors/pallas_call | solution.py:183
  22.7 1.3 %copy.7 = f32[128,4096]{1,0:T(8,128)} copy(f32[128,4096]{1,0:T(8,128)S(1)} %get-tuple-element.2) | data formatting | bytes 4194304
  24.0 1.3 %copy.8 = f32[128,4096]{1,0:T(8,128)} copy(f32[128,4096]{1,0:T(8,128)S(1)} %get-tuple-element.3) | data formatting | bytes 4194304

commit v3 on v2

v3 whole, which is shorter than its diff:
```python
import functools

import jax
import jax.numpy as jnp
from jax import lax
from jax.experimental import pallas as pl
from jax.experimental.pallas import tpu as pltpu
from jax.sharding import PartitionSpec as P

MESH = pl.DeviceIdType.MESH


def factor_kernel(S, B, units, count, len_ref, act_hbm, grad_hbm, act_tile, grad_tile, gath, tokens, part, landed,
                  read_sem, rs_send, rs_recv, z_send, z_recv, p_send, p_recv, c_send, c_recv):
    Z = B // 2
    q = lax.axis_index("seq")
    b = lax.axis_index("batch")
    z, core = b // 2, b % 2
    T, D = act_hbm.shape[1:]
    cols = D // S
    R = part.shape[2]
    sources = (act_hbm, grad_hbm)
    tiles = (act_tile, grad_tile)
    tile = act_tile.shape[0]
    U = len(units)

    def read(u, c):
        t, low, width = units[u]
        s = pl.ds(c * cols + low, width)
        return pltpu.make_async_copy(sources[t].at[0, :, s], tokens.at[t, :, s], read_sem.at[u, c])

    for u in range(U):
        for c in range(S):
            read(u, c).start()

    def seq_at(k):
        return lax.rem(q + k, S)

    def z_at(j):
        return lax.rem(z + j, Z)

    def span(owner, u):
        t, low, width = units[u]
        return pl.ds(pl.multiple_of(owner * cols + low, 128), width)

    def within(u):
        return pl.ds(units[u][1], units[u][2])

    seq_peers = [{"seq": seq_at(k)} for k in range(1, S)]
    z_peers = [{"batch": z_at(j) * 2 + core} for j in range(1, Z)]
    other = {"batch": z * 2 + 1 - core}
    barrier = pltpu.get_barrier_semaphore()
    everyone = seq_peers + z_peers + [other]
    for peer in everyone:
        pl.semaphore_signal(barrier, inc=1, device_id=peer, device_id_type=MESH)

    row = lax.broadcasted_iota(jnp.int32, (8, T), 0)
    position = q * T + lax.broadcasted_iota(jnp.int32, (8, T), 1)
    first = jnp.zeros((8, T), jnp.int32)
    last = jnp.zeros((8, T), jnp.int32)
    begin = 0
    for s in range(count):
        end = begin + len_ref[0, s]
        first = jnp.where(row == s, begin, first)
        last = jnp.where(row == s, end, last)
        begin = end
    member = ((position >= first) & (position < last)).astype(jnp.float32).astype(jnp.bfloat16)

    which = lax.broadcasted_iota(jnp.int32, (R, cols), 0)
    sizes = jnp.ones((R, cols), jnp.float32)
    for s in range(count):
        sizes = jnp.where(which == s, len_ref[0, s].astype(jnp.float32), sizes)

    def send(src, dst, send_sem, recv_sem, peer):
        return pltpu.make_async_remote_copy(
            src_ref=src, dst_ref=dst, send_sem=send_sem, recv_sem=recv_sem, device_id=peer, device_id_type=MESH)

    def scatter(u, k):
        t = units[u][0]
        return send(part.at[t, seq_at(k), :, within(u)], landed.at[t, k - 1, :, within(u)],
                    rs_send.at[u, k - 1], rs_recv.at[u, k - 1], seq_peers[k - 1])

    def scatter_to(u, c):
        t = units[u][0]
        slot = lax.rem(c - q + S, S) - 1

        @pl.when(q != c)
        def _():
            send(part.at[t, c, :, within(u)], landed.at[t, slot, :, within(u)],
                 rs_send.at[u, slot], rs_recv.at[u, slot], {"seq": jnp.int32(c)}).start()

    def at_z(u, j, zz):
        block = gath.at[units[u][0], core, zz, :, span(q, u)]
        return send(block, block, z_send.at[u, j - 1], z_recv.at[u, j - 1], z_peers[j - 1])

    def to_plane(u, k, zz):
        block = gath.at[units[u][0], core, zz, :, span(q, u)]
        return send(block, block, p_send.at[u, k - 1], p_recv.at[u, k - 1], seq_peers[k - 1])

    def plane_group(u, k, owner):
        block = gath.at[units[u][0], core, :, :, span(owner, u)]
        return send(block, block, p_send.at[u, k - 1], p_recv.at[u, k - 1], seq_peers[k - 1])

    def to_core(u, k, side):
        block = gath.at[units[u][0], side, :, :, span(seq_at(S - k), u)]
        return send(block, block, c_send.at[u, k], c_recv.at[u, k], other)

    for u, (t, low, width) in enumerate(units):
        for c in range(S):
            read(u, c).wait()
            block = tokens[t, :, c * cols + low:c * cols + low + width]
            sums = jnp.dot(member, block, preferred_element_type=jnp.float32)[:R]
            part[t, c, :, low:low + width] = sums / sizes[:, :width] if t == 0 else sums
            if u == 0 and c == 0:
                pl.semaphore_wait(barrier, len(everyone))
            scatter_to(u, c)

    for u, (t, low, width) in enumerate(units):
        total = part[t, q, :, low:low + width]
        for k in range(1, S):
            scatter(u, k).wait_recv()
            total = total + landed[t, k - 1, :, low:low + width]
        gath[t, core, z, :, span(q, u)] = total.astype(jnp.bfloat16)
        for j in range(1, Z):
            at_z(u, j, z).start()
        for k in range(1, S):
            to_plane(u, k, z).start()

    for u in range(U):
        for j in range(1, Z):
            at_z(u, j, z_at(Z - j)).wait_recv()
            for k in range(1, S):
                to_plane(u, k, z_at(Z - j)).start()
        to_core(u, 0, core).start()

    K = 2 * Z * R

    def rows(t, s):
        return gath[t, :, :, :, s].reshape(K, -1)

    wide = max(tile, 128)
    at = q * cols + b * tile

    for t in range(2):
        mine = [u for u in range(U) if units[u][0] == t]

        for u in mine:
            for k in range(1, S):
                plane_group(u, k, seq_at(S - k)).wait_recv()
                to_core(u, k, core).start()
        for u in mine:
            for k in range(S):
                to_core(u, k, 1 - core).wait_recv()

        if tile % 128 == 0:
            block = rows(t, pl.ds(pl.multiple_of(at, 128), tile))
        else:
            block = rows(t, pl.ds(pl.multiple_of(at // wide * wide, wide), wide))
            pick = lax.broadcasted_iota(jnp.int32, (wide, tile), 0) == at % wide + lax.broadcasted_iota(jnp.int32, (wide, tile), 1)
            block = jnp.dot(block, pick.astype(jnp.float32).astype(jnp.bfloat16), preferred_element_type=jnp.float32).astype(jnp.bfloat16)
        left = block.T
        for c in range(S):
            s = slice(c * cols, (c + 1) * cols)
            tiles[t][:, s] = jnp.dot(left, rows(t, s), preferred_element_type=jnp.float32) * (1.0 / (count * B))

    for u in range(U):
        for k in range(S):
            to_core(u, k, core).wait_send()
        for k in range(1, S):
            plane_group(u, k, q).wait_send()
            scatter(u, k).wait_send()
        for j in range(1, Z):
            at_z(u, j, z).wait_send()


def put_kernel(steps, act_tile, grad_tile, act_out, grad_out, sem):
    step = act_tile.shape[1] // steps
    copies = [pltpu.make_async_copy(src.at[:, pl.ds(i * step, step)], dst.at[:, pl.ds(i * step, step)], sem.at[t, i])
              for t, (src, dst) in enumerate(((act_tile, act_out), (grad_tile, grad_out))) for i in range(steps)]
    for copy in copies:
        copy.start()
    for copy in copies:
        copy.wait()


def solution(mesh):
    S, B = mesh.shape["seq"], mesh.shape["batch"]
    Z = B // 2

    def local(activations, out_grads, lengths):
        T, D = activations.shape[1:]
        count = lengths.shape[1]
        R = max(2, 1 << (count - 1).bit_length())
        cols = D // S
        tile = D // (S * B)
        half = cols // 2
        units = ((0, 0, cols), (1, 0, half), (1, half, half))
        U = len(units)
        out = pltpu.VMEM((tile, D), jnp.float32)
        tiles = pl.pallas_call(
            functools.partial(factor_kernel, S, B, units, count),
            out_shape=(out, out),
            in_specs=[pl.BlockSpec(memory_space=pltpu.SMEM), pl.BlockSpec(memory_space=pl.ANY), pl.BlockSpec(memory_space=pl.ANY)],
            out_specs=(pl.BlockSpec(memory_space=pltpu.VMEM), pl.BlockSpec(memory_space=pltpu.VMEM)),
            scratch_shapes=[
                pltpu.VMEM((2, 2, Z, R, D), jnp.bfloat16),
                pltpu.VMEM((2, T, D), jnp.bfloat16),
                pltpu.VMEM((2, S, R, cols), jnp.float32),
                pltpu.VMEM((2, S - 1, R, cols), jnp.float32),
                pltpu.SemaphoreType.DMA((U, S)),
                pltpu.SemaphoreType.DMA((U, S - 1)),
                pltpu.SemaphoreType.DMA((U, S - 1)),
                pltpu.SemaphoreType.DMA((U, Z - 1)),
                pltpu.SemaphoreType.DMA((U, Z - 1)),
                pltpu.SemaphoreType.DMA((U, S - 1)),
                pltpu.SemaphoreType.DMA((U, S - 1)),
                pltpu.SemaphoreType.DMA((U, S)),
                pltpu.SemaphoreType.DMA((U, S)),
            ],
            compiler_params=pltpu.CompilerParams(collective_id=0, has_side_effects=True, vmem_limit_bytes=56 * 2**20),
            name="factors",
        )(lengths, activations, out_grads)
        steps = 4
        held = jax.ShapeDtypeStruct((tile, D), jnp.float32)
        return tuple(pl.pallas_call(
            functools.partial(put_kernel, steps),
            out_shape=(held, held),
            in_specs=[pl.BlockSpec(memory_space=pltpu.VMEM)] * 2,
            out_specs=(pl.BlockSpec(memory_space=pl.ANY), pl.BlockSpec(memory_space=pl.ANY)),
            scratch_shapes=[pltpu.SemaphoreType.DMA((2, steps))],
            compiler_params=pltpu.CompilerParams(vmem_limit_bytes=16 * 2**20),
            name="put_tiles",
        )(*tiles))

    in_specs = (P("batch", "seq", None), P("batch", "seq", None), P("batch", None))
    out_specs = (P(("seq", "batch"), None), P(("seq", "batch"), None))
    return jax.shard_map(local, mesh=mesh, in_specs=in_specs, out_specs=out_specs, check_vma=False)
```

time: 25.5 us -> 24.3 us (0.953)
  local copies, waits for them, and re-layouts: 2.64 us -> 0 us
  Pallas kernels: 22.1 us -> 23.6 us
    unnamed x2 -> x0, local copies, waits for them, and re-layouts: 2.64 us -> none
    pallas_call x1 -> x2, Pallas kernels: 22.1 us -> 23.6 us  [the longest x1 21.5 us: local(): pl.pallas_call(functools.partial(factor_kernel, S, B, units, count), out_...]
where the time goes in v3:
time: 24.3 us; the launch traced here: 24.2 us
  Pallas kernels  23.6 us (97%)
  between operations  0.64 us (3%)
    pallas_call x1, Pallas kernels, local(): pl.pallas_call(functools.partial(factor_kernel, S, B, units, count), out_...  21.5 us
    pallas_call x1, Pallas kernels, local(): pl.pallas_call(functools.partial(put_kernel, steps), out_shape=(held, hel...  2.07 us

profile of v3, /device:TPU:0, one launch (start us, length us, event | category | flops | bytes accessed | tf_op | source)
XLA Modules:
  0.0 24.2 jit_solution(15148927439295044188)
XLA Ops:
  0.6 21.5 %factors.1 = (f32[128,4096]{1,0:T(8,128)S(1)}, f32[128,4096]{1,0:T(8,128)S(1)}) custom-call(s32[1,3]{1,0:T(1,128)} %len_ref.1, bf16[1,768,4096]{2,1,0:T(8,128)(2,1)} %act_hbm.1, bf16[1,768,4096]{2,1,0:T(8,128)(2,1)} %grad_hbm.1), custom_call_target="tpu_custom_call" | custom-call | tf_op jit(solution)/shard_map/factors/pallas_call | solution.py:200
  22.1 2.1 %put_tiles.1 = (f32[128,4096]{1,0:T(8,128)}, f32[128,4096]{1,0:T(8,128)}) custom-call(f32[128,4096]{1,0:T(8,128)S(1)} %get-tuple-element.4.act_tile, f32[128,4096]{1,0:T(8,128)S(1)} %get-tuple-element.5.grad_tile), custom_call_target="tpu_custom_call" | custom-call | tf_op jit(solution)/shard_map/put_tiles/pallas_call | solution.py:225
